TPU v7x, 32 devices: a whole 2x2x4 slice. The times are simulated.
32 devices in a mesh: types: 16 (over z, y, x), tm: 2 (over core).
Axes of the slice: x: 2, y: 2, z: 4, core: 2. Of those that a mesh axis runs over, the one named last changes fastest.
Arguments:
- brackets: int32 [96, 8, 7, 512], P('types', 'tm'), may hold values from 0 to 510, as said below
- active_blocks: int32 [96], P('types'), may hold values from 1 to 4, as said below
- initial_mass: float32 [96, 7, 512], P('types'), may hold values from 0 to 0.00055803574
- patience: float32 [96], P('types'), may hold values from 0.9 to 0.985
- productivity: float32 [96], P('types'), may hold values from 0.5 to 2
- income_levels: float32 [7], replicated, may hold values from 0.3 to 3
- income_transition: float32 [7, 7], replicated, may hold values from 0 to 1, as said below
- wage_path: float32 [8], replicated, may hold values from 0.8 to 1.2
- bond_supply: float32 [8], replicated, may hold values from 0.5 to 2
- price_guess: float32 [8], replicated, may hold values from -3 to 3
- jac_inverse: float32 [8, 8], replicated, may hold values from -2 to 2
- assignment: int32 [96], replicated, may hold values from 0 to 95, each once
Outputs:
- price_path: float32 [8], replicated
- market_gap: float32 [8], replicated
- type_paths: float32 [96, 2, 8], P('types')
Inputs may be any that keep to these rules, and one draw needn't show every extreme that they name: `brackets`: the bracket of asset point i lies between max(i - 9, 0) and max(i - 1, 0). `active_blocks`: counts of 128-point blocks from the bottom of the grid. `income_transition`: rows of positive entries summing to one. `assignment`: each type appears once.
All inputs are finite; a program needn't handle non-finite values.
Results may differ from a plain program's by a relative error of at most 0.0003.
Values sent between devices are 32-bit elements; how exact they have to be, the bound alone decides.
A program may use at most 64 MiB of HBM per device.

v0:
```python
import jax
import jax.numpy as jnp
from jax import lax
from jax.sharding import PartitionSpec as P

ASSETS = 512
BLOCK = 128
NEWTON = 2


grid_top = 40.0
rate_floor = 0.005
rate_span = 0.03
highest = lax.Precision.HIGHEST


def asset_grid(points):
    return grid_top * (points / (ASSETS - 1)) ** 2


def interest(price_path):
    return rate_floor + rate_span * jax.nn.sigmoid(price_path)


def policy(lower_edge, upper_edge, bracket_now, rate_now, income_now, grid_rows):
    grid_low = asset_grid(bracket_now.astype(jnp.float32))
    grid_high = asset_grid((bracket_now + 1).astype(jnp.float32))
    spacing = jnp.maximum(upper_edge - lower_edge, (grid_high - grid_low) / (1.0 + rate_now))
    weight_up = jnp.clip((grid_rows[None, :] - lower_edge) / spacing, 0.0, 1.0)
    savings = grid_low + weight_up * (grid_high - grid_low)
    spending = (1.0 + rate_now) * grid_rows[None, :] + income_now[:, None] - savings
    return (weight_up, savings, spending)


def band_table(bracket_rows, window):
    targets = window + jnp.arange(2 * BLOCK, dtype=jnp.int32)
    return (bracket_rows[:, :, None] == targets[None, None, :]).astype(jnp.float32)


def backward_type(bracket, blocks, patience, incomes, interest_path, values_end, transition):
    grid_values = asset_grid(jnp.arange(ASSETS, dtype=jnp.float32))
    income_count = values_end.shape[0]

    def backward_period(values, inputs):
        bracket_now, rate_now, income_now = inputs
        expected = patience * jnp.dot(transition, values, precision=highest)
        endogenous = (1.0 / expected + grid_values[None, :] - income_now[:, None]) / (
            1.0 + rate_now
        )
        following = jnp.concatenate([endogenous[:, 1:], endogenous[:, -1:]], axis=1)
        stacked = jnp.stack([endogenous, following])

        def backward_block_rows(block_index, carried):
            row_start = block_index * BLOCK
            window = jnp.maximum(row_start - BLOCK, 0)
            bracket_rows = lax.dynamic_slice_in_dim(bracket_now, row_start, BLOCK, 1)
            onehot = band_table(bracket_rows, window)
            stacked_window = lax.dynamic_slice_in_dim(stacked, window, 2 * BLOCK, 2)
            picked = jnp.einsum("eia,cea->cei", onehot, stacked_window, precision=highest)
            grid_rows = lax.dynamic_slice_in_dim(grid_values, row_start, BLOCK, 0)
            weight_up, savings, spending = policy(
                picked[0], picked[1], bracket_rows, rate_now, income_now, grid_rows
            )
            fresh = (weight_up, savings, spending, (1.0 + rate_now) / spending)
            return tuple(
                (
                    lax.dynamic_update_slice_in_dim(target_array, piece_array, row_start, 1)
                    for target_array, piece_array in zip(carried, fresh)
                )
            )

        zeros_rows = jnp.zeros((income_count, ASSETS), jnp.float32)
        ones_rows = jnp.ones((income_count, ASSETS), jnp.float32)
        weight_up, savings, spending, values_new = lax.fori_loop(
            0, blocks, backward_block_rows, (zeros_rows, zeros_rows, ones_rows, ones_rows)
        )
        return (values_new, (weight_up, savings, spending))

    return lax.scan(backward_period, values_end, (bracket, interest_path, incomes), reverse=True)


def forward_type(bracket, blocks, weight_up, savings, spending, mass_start, transition):

    def forward_period(masses, inputs):
        bracket_now, weight_now, savings_now, spending_now = inputs
        totals = jnp.stack([jnp.sum(masses * savings_now), jnp.sum(masses * spending_now)])
        weights = jnp.stack([(1.0 - weight_now) * masses, weight_now * masses])

        def forward_block_rows(block_index, shifted_mass):
            row_start = block_index * BLOCK
            window = jnp.maximum(row_start - BLOCK, 0)
            bracket_rows = lax.dynamic_slice_in_dim(bracket_now, row_start, BLOCK, 1)
            onehot = band_table(bracket_rows, window)
            weight_rows = lax.dynamic_slice_in_dim(weights, row_start, BLOCK, 2)
            contrib = jnp.einsum("eia,cei->cea", onehot, weight_rows, precision=highest)
            current = lax.dynamic_slice_in_dim(shifted_mass, window, 2 * BLOCK, 2)
            return lax.dynamic_update_slice_in_dim(shifted_mass, current + contrib, window, 2)

        shifted_mass = lax.fori_loop(0, blocks, forward_block_rows, jnp.zeros_like(weights))
        arrived = shifted_mass[0] + jnp.concatenate(
            [jnp.zeros_like(shifted_mass[1][:, :1]), shifted_mass[1][:, :-1]], axis=1
        )
        return (jnp.dot(transition.T, arrived, precision=highest), totals)

    masses_end, type_series = lax.scan(
        forward_period, mass_start, (bracket, weight_up, savings, spending)
    )
    return (masses_end, type_series.T)


def body(
    brackets,
    active_blocks,
    initial_mass,
    patience,
    productivity,
    income_levels,
    income_transition,
    wage_path,
    bond_supply,
    price_guess,
    jac_inverse,
    assignment,
):
    local_types = patience.shape[0]
    all_types = local_types * lax.axis_size("types")
    core_count = lax.axis_size("tm")
    core_index = lax.axis_index("tm")
    columns = jnp.arange(ASSETS, dtype=jnp.int32)
    grid_values = asset_grid(columns.astype(jnp.float32))
    type_numbers = (
        lax.axis_index("types") * local_types + jnp.arange(local_types, dtype=jnp.int32)
    ).astype(jnp.float32)
    half_types = local_types // core_count
    brackets_mine = lax.all_to_all(brackets, "tm", split_axis=0, concat_axis=1, tiled=True)

    def take_mine(target_array):
        return lax.dynamic_slice_in_dim(target_array, core_index * half_types, half_types, 0)

    blocks_mine = take_mine(active_blocks)
    patience_mine = take_mine(patience)
    productivity_mine = take_mine(productivity)
    mass_mine = take_mine(initial_mass)
    numbers_mine = take_mine(type_numbers)
    live_rows = (columns[None, None, :] < blocks_mine[:, None, None] * BLOCK).astype(jnp.float32)
    mass_start = mass_mine * live_rows
    price_path = price_guess
    market_gap = jnp.zeros_like(price_guess)
    everything = None
    for newton_round in range(NEWTON):
        interest_path = interest(price_path)
        last_rate = interest_path[-1]
        ends_income = wage_path[-1] * productivity_mine[:, None] * income_levels[None, :]
        values_end = (1.0 + last_rate) / (
            last_rate * grid_values[None, None, :] + ends_income[:, :, None]
        )
        interest_here = interest_path
        incomes = (
            wage_path[None, :, None]
            * productivity_mine[:, None, None]
            * income_levels[None, None, :]
        )

        def sweep_solve_member(members):
            return backward_type(
                members[0],
                members[1],
                members[2],
                members[3],
                interest_here,
                members[4],
                income_transition,
            )

        values_start, solve_policies = lax.map(
            sweep_solve_member, (brackets_mine, blocks_mine, patience_mine, incomes, values_end)
        )

        def solve_member(members):
            return forward_type(
                members[0],
                members[1],
                members[2],
                members[3],
                members[4],
                members[5],
                income_transition,
            )

        masses_end, solve_type_series = lax.map(
            solve_member,
            (
                brackets_mine,
                blocks_mine,
                solve_policies[0],
                solve_policies[1],
                solve_policies[2],
                mass_start,
            ),
        )
        local_sum = jnp.sum(solve_type_series[:, 0, :], axis=0)
        totals = lax.psum(local_sum, ("types", "tm"))
        if newton_round + 1 == NEWTON:
            everything = (
                lax.all_gather(solve_type_series, ("types", "tm"), axis=0, tiled=True),
                lax.all_gather(numbers_mine, ("types", "tm"), axis=0, tiled=True),
            )
        market_gap = totals / all_types - bond_supply
        price_path = price_path - jnp.dot(jac_inverse, market_gap, precision=highest)
    slot_types = lax.dynamic_slice_in_dim(
        assignment, lax.axis_index("types") * local_types, local_types, 0
    ).astype(jnp.float32)
    select = (slot_types[:, None] == everything[1][None, :]).astype(jnp.float32)
    type_paths = jnp.einsum("st,tcp->scp", select, everything[0], precision=highest)
    return (price_path, market_gap, type_paths)


def solution(mesh):
    placed = (
        P("types", "tm", None, None),
        P("types"),
        P("types", None, None),
        P("types"),
        P("types"),
        P(),
        P(),
        P(),
        P(),
        P(),
        P(),
        P(),
    )
    return jax.shard_map(
        body,
        mesh=mesh,
        in_specs=placed,
        out_specs=(P(), P(), P("types", None, None)),
        check_vma=False,
    )
```

profile of v0, /device:TPU:0, one launch (start us, length us, event | category | flops | bytes accessed | tf_op | source)
XLA Modules:
  0.0 990.3 jit_solution(13439941722664523661)
XLA Ops:
  12.0 195.2 %while.321 = (s32[]{:T(128)}, f32[3,8,7,512]{3,2,1,0:T(8,128)S(1)}, f32[3,8,7,512]{3,2,1,0:T(8,128)S(1)}, f32[3,8,7,512]{3,2,1,0:T(8,128)S(1)}, f32[3,7,512]{2,1...) while((s32[]{:T(128)}, f32[3,8,7,512]{3,2,1,0:T(8,128)S(1)}, ...), condition=%wide.region_5.6_spmd, body=%wide.region_0.5_spmd.sunk | while | flops 6097422 | bytes 1872705 | solution.py:175
  13.4 59.6 %while.328 = (s32[]{:T(128)}, f32[7,512]{1,0:T(8,128)S(1)}, f32[8,7,512]{2,1,0:T(8,128)S(1)}, f32[8,7,512]{2,1,0:T(8,128)S(1)}, f32[8,7,512]{2,1,0:T(8,128)S(1)}...) while((s32[]{:T(128)}, f32[7,512]{1,0:T(8,128)S(1)}, ...), condition=%wide.region_4.4_spmd.clone.clone, body=%wide.region_1.3_spmd.clone.clone.sunk | while | flops 6097420 | bytes 483244 | solution.py:79
  74.5 59.6 %while.328 = (s32[]{:T(128)}, f32[7,512]{1,0:T(8,128)S(1)}, f32[8,7,512]{2,1,0:T(8,128)S(1)}, f32[8,7,512]{2,1,0:T(8,128)S(1)}, f32[8,7,512]{2,1,0:T(8,128)S(1)}...) while((s32[]{:T(128)}, f32[7,512]{1,0:T(8,128)S(1)}, ...), condition=%wide.region_4.4_spmd.clone.clone, body=%wide.region_1.3_spmd.clone.clone.sunk | while | flops 6097420 | bytes 483244 | solution.py:79
  135.6 71.5 %while.328 = (s32[]{:T(128)}, f32[7,512]{1,0:T(8,128)S(1)}, f32[8,7,512]{2,1,0:T(8,128)S(1)}, f32[8,7,512]{2,1,0:T(8,128)S(1)}, f32[8,7,512]{2,1,0:T(8,128)S(1)}...) while((s32[]{:T(128)}, f32[7,512]{1,0:T(8,128)S(1)}, ...), condition=%wide.region_4.4_spmd.clone.clone, body=%wide.region_1.3_spmd.clone.clone.sunk | while | flops 6097420 | bytes 483244 | solution.py:79
  137.9 6.6 while.335
  146.9 6.6 while.335
  155.8 6.6 while.335
  164.7 6.6 while.335
  173.7 6.6 while.335
  182.6 6.6 while.335
  191.6 6.6 while.335
  200.5 6.6 while.335
  207.3 187.7 %while.323 = (s32[]{:T(128)}, f32[3,2,8]{2,1,0:T(2,128)S(1)}, f32[3,7,512]{2,1,0:T(8,128)S(1)}, s32[3,8,7,512]{3,2,1,0:T(8,128)S(1)}, f32[3,8,7,512]{3,2,1,0:T(8...) while((s32[]{:T(128)}, f32[3,2,8]{2,1,0:T(2,128)S(1)}, ...), condition=%wide.region_13.14_spmd, body=%wide.region_6.13_spmd.sunk | while | flops 6075148 | bytes 1450953 | solution.py:190
  208.0 58.1 %while.329 = (s32[]{:T(128)}, f32[7,512]{1,0:T(8,128)S(1)}, f32[8,2]{1,0:T(8,128)S(1)}, s32[8,7,512]{2,1,0:T(8,128)S(1)}, f32[8,7,512]{2,1,0:T(8,128)S(1)}, /*in...) while((s32[]{:T(128)}, f32[7,512]{1,0:T(8,128)S(1)}, ...), condition=%wide.region_12.12_spmd, body=%wide.region_7.11_spmd.sunk | while | flops 6075146 | bytes 502252 | solution.py:105
  266.9 58.1 %while.329 = (s32[]{:T(128)}, f32[7,512]{1,0:T(8,128)S(1)}, f32[8,2]{1,0:T(8,128)S(1)}, s32[8,7,512]{2,1,0:T(8,128)S(1)}, f32[8,7,512]{2,1,0:T(8,128)S(1)}, /*in...) while((s32[]{:T(128)}, f32[7,512]{1,0:T(8,128)S(1)}, ...), condition=%wide.region_12.12_spmd, body=%wide.region_7.11_spmd.sunk | while | flops 6075146 | bytes 502252 | solution.py:105
  325.8 69.1 %while.329 = (s32[]{:T(128)}, f32[7,512]{1,0:T(8,128)S(1)}, f32[8,2]{1,0:T(8,128)S(1)}, s32[8,7,512]{2,1,0:T(8,128)S(1)}, f32[8,7,512]{2,1,0:T(8,128)S(1)}, /*in...) while((s32[]{:T(128)}, f32[7,512]{1,0:T(8,128)S(1)}, ...), condition=%wide.region_12.12_spmd, body=%wide.region_7.11_spmd.sunk | while | flops 6075146 | bytes 502252 | solution.py:105
  326.5 6.2 while.334
  335.2 6.2 while.334
  343.8 6.2 while.334
  352.5 6.2 while.334
  361.1 6.2 while.334
  378.4 6.2 while.334
  387.0 6.2 while.334
  395.0 87.6 %psum.14 = f32[8]{0:T(128)S(1)} all-reduce(f32[8]{0:T(128)S(1)} %slice_reduce_fusion.1), channel_id=1, replica_groups=mesh['types'=16,'tm'=2] {'types','tm'}, use_global_device_ids=true, to_apply=%region_15.16 | all-reduce | flops 8 | bytes 64 | tf_op jit(solution)/shard_map/psum | solution.py:202
  484.9 195.2 %while.325 = (s32[]{:T(128)}, f32[3,8,7,512]{3,2,1,0:T(8,128)S(1)}, f32[3,8,7,512]{3,2,1,0:T(8,128)S(1)}, f32[3,8,7,512]{3,2,1,0:T(8,128)S(1)}, f32[3,7,512]{2,1...) while((s32[]{:T(128)}, f32[3,8,7,512]{3,2,1,0:T(8,128)S(1)}, ...), condition=%wide.region_21.22_spmd, body=%wide.region_16.21_spmd.sunk | while | flops 6097422 | bytes 1872697 | solution.py:175
  486.3 59.6 %while.330 = (s32[]{:T(128)}, f32[7,512]{1,0:T(8,128)S(1)}, f32[8,7,512]{2,1,0:T(8,128)S(1)}, f32[8,7,512]{2,1,0:T(8,128)S(1)}, f32[8,7,512]{2,1,0:T(8,128)S(1)}...) while((s32[]{:T(128)}, f32[7,512]{1,0:T(8,128)S(1)}, ...), condition=%wide.region_20.20_spmd.clone.clone, body=%wide.region_17.19_spmd.clone.clone.sunk | while | flops 6097420 | bytes 483244 | solution.py:79
  547.4 59.6 %while.330 = (s32[]{:T(128)}, f32[7,512]{1,0:T(8,128)S(1)}, f32[8,7,512]{2,1,0:T(8,128)S(1)}, f32[8,7,512]{2,1,0:T(8,128)S(1)}, f32[8,7,512]{2,1,0:T(8,128)S(1)}...) while((s32[]{:T(128)}, f32[7,512]{1,0:T(8,128)S(1)}, ...), condition=%wide.region_20.20_spmd.clone.clone, body=%wide.region_17.19_spmd.clone.clone.sunk | while | flops 6097420 | bytes 483244 | solution.py:79
  608.5 71.5 %while.330 = (s32[]{:T(128)}, f32[7,512]{1,0:T(8,128)S(1)}, f32[8,7,512]{2,1,0:T(8,128)S(1)}, f32[8,7,512]{2,1,0:T(8,128)S(1)}, f32[8,7,512]{2,1,0:T(8,128)S(1)}...) while((s32[]{:T(128)}, f32[7,512]{1,0:T(8,128)S(1)}, ...), condition=%wide.region_20.20_spmd.clone.clone, body=%wide.region_17.19_spmd.clone.clone.sunk | while | flops 6097420 | bytes 483244 | solution.py:79
  610.8 6.6 while.333
  619.7 6.6 while.333
  628.7 6.6 while.333
  637.6 6.6 while.333
  646.6 6.6 while.333
  655.5 6.6 while.333
  664.5 6.6 while.333
  673.4 6.6 while.333
  680.1 187.7 %while.327 = (s32[]{:T(128)}, f32[3,2,8]{2,1,0:T(2,128)S(1)}, f32[3,7,512]{2,1,0:T(8,128)S(1)}, s32[3,8,7,512]{3,2,1,0:T(8,128)S(1)}, f32[3,8,7,512]{3,2,1,0:T(8...) while((s32[]{:T(128)}, f32[3,2,8]{2,1,0:T(2,128)S(1)}, ...), condition=%wide.region_29.30_spmd, body=%wide.region_22.29_spmd.sunk | while | flops 6075148 | bytes 1450953 | solution.py:190
  680.8 58.1 %while.331 = (s32[]{:T(128)}, f32[7,512]{1,0:T(8,128)S(1)}, f32[8,2]{1,0:T(8,128)S(1)}, s32[8,7,512]{2,1,0:T(8,128)S(1)}, f32[8,7,512]{2,1,0:T(8,128)S(1)}, /*in...) while((s32[]{:T(128)}, f32[7,512]{1,0:T(8,128)S(1)}, ...), condition=%wide.region_28.28_spmd, body=%wide.region_23.27_spmd.sunk | while | flops 6075146 | bytes 502252 | solution.py:105
  739.7 58.1 %while.331 = (s32[]{:T(128)}, f32[7,512]{1,0:T(8,128)S(1)}, f32[8,2]{1,0:T(8,128)S(1)}, s32[8,7,512]{2,1,0:T(8,128)S(1)}, f32[8,7,512]{2,1,0:T(8,128)S(1)}, /*in...) while((s32[]{:T(128)}, f32[7,512]{1,0:T(8,128)S(1)}, ...), condition=%wide.region_28.28_spmd, body=%wide.region_23.27_spmd.sunk | while | flops 6075146 | bytes 502252 | solution.py:105
  798.6 69.1 %while.331 = (s32[]{:T(128)}, f32[7,512]{1,0:T(8,128)S(1)}, f32[8,2]{1,0:T(8,128)S(1)}, s32[8,7,512]{2,1,0:T(8,128)S(1)}, f32[8,7,512]{2,1,0:T(8,128)S(1)}, /*in...) while((s32[]{:T(128)}, f32[7,512]{1,0:T(8,128)S(1)}, ...), condition=%wide.region_28.28_spmd, body=%wide.region_23.27_spmd.sunk | while | flops 6075146 | bytes 502252 | solution.py:105
  799.4 6.2 while.332
  808.0 6.2 while.332
  816.6 6.2 while.332
  833.9 6.2 while.332
  842.6 6.2 while.332
  851.2 6.2 while.332
  867.8 83.0 %all_gather.7 = f32[96,2,8]{2,1,0:T(2,128)S(1)} all-gather(f32[3,2,8]{2,1,0:T(2,128)S(1)} %get-tuple-element.1994), channel_id=1, replica_groups=mesh['types'=16,'tm'=2] {'types','tm'}, dimensions={0}, use_global_device_ids=true | all-gather | bytes 6336 | tf_op jit(solution)/shard_map/all_gather | solution.py:205
  950.8 36.8 %all-reduce.3 = (f32[8]{0:T(128)S(1)}, f32[96]{0:T(128)S(1)}) all-reduce(f32[8]{0:T(128)S(1)} %slice_reduce_fusion, f32[96]{0:T(128)S(1)} %get-tuple-element.2439), channel_id=1, replica_groups=mesh['types'=16,'tm'=2] {'types','tm'}, use_global_device_ids=true, to_apply=%region_31.32 | all-reduce | flops 104 | bytes 832 | tf_op jit(solution)/shard_map/psum | solution.py:202
  (3340 shorter events, 794.8 us)
Async XLA Ops:
  0.6 482.0 %copy-start = (f32[8,8]{1,0:T(8,128)S(1)}, f32[8,8]{1,0:T(8,128)}, u32[]{:S(2)}) copy-start(f32[8,8]{1,0:T(8,128)} %param.46) | copy-start | bytes 772
  0.6 10.4 %all-to-all-start = ((s32[6,4,7,512]{3,1,2,0:T(4,128)}), s32[6,4,7,512]{3,1,2,0:T(4,128)S(1)}, u32[]{:S(2)}, u32[]{:S(2)}) async-start(s32[6,4,7,512]{3,1,2,0:T(4,128)} %param.36), calls=%async_computation | async-start | bytes 688128 | tf_op jit(solution)/shard_map/all_to_all | solution.py:135
  4.1 0.7 copy-start.3
  4.8 0.7 copy-start.8
  7.4 0.7 copy-start.5
  8.9 0.7 copy-start.2
  9.6 0.7 copy-start.4
  10.3 0.7 copy-start.7
  11.3 0.7 copy-start.6
  12.0 195.3 %copy-start.1 = (f32[6,7,512]{2,1,0:T(8,128)S(1)}, f32[6,7,512]{2,1,0:T(8,128)}, u32[]{:S(2)}) copy-start(f32[6,7,512]{2,1,0:T(8,128)} %param.38) | copy-start | bytes 258052
  395.0 87.6 %copy-start.10 = (f32[8]{0:T(128)S(1)}, f32[8]{0:T(128)}, u32[]{:S(2)}) copy-start(f32[8]{0:T(128)} %param.44) | copy-start | bytes 100
  987.6 0.7 copy-start.9
  989.2 0.5 copy-start.11
where the time goes:
time: 973 us; the launch traced here: 990 us
  loops' own time  321 us (33%)
  blocking collectives  207 us (21%)
  matrix products  204 us (21%)
  other arithmetic  140 us (14%)
  local copies, waits for them, and re-layouts  111 us (11%)
    another operation x48, loops' own time, forward_period(): lax.fori_loop(0, blocks, forward_block_rows, jnp.zeros_like(weights))  144 us
    another operation x48, loops' own time, backward_period(): lax.fori_loop(0, blocks, backward_block_rows, (zeros_rows, zeros_rows, on...  140 us
    psum x2, blocking collectives, body(): totals = lax.psum(local_sum, ('types', 'tm'))  124 us
    dot_general x160, matrix products, backward_block_rows(): jnp.einsum('eia,cea->cei', onehot, stacked_window, precision=highest)  88.8 us
    all_gather x1, blocking collectives, body(): lax.all_gather(solve_type_series, ('types', 'tm'), axis=0, tiled=True)  83 us
    dot_general x160, matrix products, forward_block_rows(): contrib = jnp.einsum('eia,cei->cea', onehot, weight_rows, precision=highest)  66.5 us
    broadcast_in_dim x48, other arithmetic, forward_type(): lax.scan(forward_period, mass_start, (bracket, weight_up, savings, spendi...  64.1 us
    dynamic_update_slice x160, local copies, waits for them, and re-layouts, forward_block_rows(): lax.dynamic_update_slice_in_dim(shifted_mass, current + contrib, window, 2)  41.4 us
  transfers between devices with their start and end apart: 1, of which 0 were waited for; matrix products, arithmetic and copies ran while one was open for 0% of the time, Pallas kernels for 0%

commit v1 on v0

v1 whole, which is shorter than its diff:
```python
import functools

import jax
import jax.numpy as jnp
from jax import lax
from jax.experimental import pallas as pl
from jax.experimental.pallas import tpu as pltpu
from jax.sharding import PartitionSpec as P

BLOCK = 128
REACH = 8
NEWTON = 2
ROWS = 8
LANES = 128

grid_top = 40.0
rate_floor = 0.005
rate_span = 0.03
MESH = pl.DeviceIdType.MESH


def iota(axis):
    return lax.broadcasted_iota(jnp.int32, (ROWS, LANES), axis)


def take(source, index):
    return jnp.take_along_axis(source, index, axis=1, mode="promise_in_bounds")


def to_column(row):
    spread = jnp.where(iota(0) == iota(1), jnp.broadcast_to(row, (ROWS, LANES)), 0.0)
    return jnp.sum(spread, axis=1, keepdims=True)


def to_row(column, offset):
    spread = jnp.where(iota(0) + offset == iota(1), jnp.broadcast_to(column, (ROWS, LANES)), 0.0)
    return jnp.sum(spread, axis=0, keepdims=True)


def shifted(row, lanes):
    return row if lanes == 0 else pltpu.roll(row, LANES - lanes, 1)


def kernel(
    sizes,
    brackets, active, initial_mass, patience, productivity, levels, transition,
    wage, bond, price_in, jac, assignment,
    price_out, gap_out, paths_out,
    br, mass_in, vals, mass, arrived, weights, savings, spending, totals,
    t_back, t_fwd, level_col, rates, send_row, recv_a, recv_b,
    br_sem, br_send, mass_sem, row_send, row_recv,
):
    groups, cores, local_types, periods, incomes, assets = sizes
    mine = local_types // cores
    here = periods // cores
    blocks = assets // LANES
    devices = groups * cores
    group = lax.axis_index("types")
    core = lax.axis_index("tm")
    me = group * cores + core
    grid_unit = grid_top / float(assets - 1) ** 2

    def place(flat):
        return (flat // cores, lax.rem(flat, cores))

    def local_copy(p):
        return pltpu.make_async_copy(
            brackets.at[pl.ds(core * mine, mine), p],
            br.at[core * here + p],
            br_sem.at[core * here + p],
        )

    for p in reversed(range(here)):
        local_copy(p).start()
    mass_copy = pltpu.make_async_copy(
        initial_mass.at[pl.ds(core * mine, mine)],
        mass_in,
        mass_sem.at[0],
    )
    mass_copy.start()

    barrier = pltpu.get_barrier_semaphore()

    def greet(o, carry):
        pl.semaphore_signal(
            barrier, inc=1, device_id=place(lax.rem(me + o, devices)), device_id_type=MESH
        )
        return carry

    lax.fori_loop(1, devices, greet, 0)

    row_id = iota(0)
    lane_id = iota(1)
    for f in range(incomes):
        back = jnp.full((ROWS, LANES), 1.0 / incomes, jnp.float32)
        ahead = jnp.zeros((ROWS, LANES), jnp.float32)
        for e in range(incomes):
            back = jnp.where(row_id == e, transition[e, f], back)
            ahead = jnp.where(row_id == e, transition[f, e], ahead)
        t_back[f] = back
        t_fwd[f] = ahead
    column = jnp.ones((ROWS, LANES), jnp.float32)
    for e in range(incomes):
        column = jnp.where(row_id == e, levels[e], column)
    level_col[...] = column

    pl.semaphore_wait(barrier, devices - 1)

    def peer_copy(o, p):
        peer = lax.rem(core + o, cores)
        return pltpu.make_async_remote_copy(
            src_ref=brackets.at[pl.ds(peer * mine, mine), p],
            dst_ref=br.at[core * here + p],
            send_sem=br_send.at[o - 1, p],
            recv_sem=br_sem.at[core * here + p],
            device_id=(group, peer),
            device_id_type=MESH,
        )

    for p in reversed(range(here)):
        for o in range(1, cores):
            peer_copy(o, p).start()

    def grid_block(b):
        point = (lane_id + b * LANES).astype(jnp.float32)
        return grid_unit * (point * point)

    def full_rows(x):
        return jnp.pad(x, ((0, ROWS - incomes), (0, 0)))

    def lanes(b):
        return pl.ds(b * LANES, LANES)

    def bracket_block(t, k, b):
        return full_rows(br[t, k, :, lanes(b)])

    price = jnp.pad(price_in[...], ((0, 0), (0, LANES - periods)))
    bond_row = jnp.pad(bond[...], ((0, 0), (0, LANES - periods)))
    mass_copy.wait()

    for newton_round in range(NEWTON):
        last = newton_round + 1 == NEWTON
        rate_row = rate_floor + rate_span / (1.0 + jnp.exp(-price))
        rate_col = jnp.broadcast_to(to_column(rate_row), (ROWS, LANES))
        rates[0] = 1.0 + rate_col
        rates[1] = 1.0 / (1.0 + rate_col)
        end_gross = jnp.broadcast_to(rates[0, pl.ds(periods - 1, 1), :], (ROWS, LANES))
        end_rate = jnp.broadcast_to(rate_col[periods - 1 : periods, :], (ROWS, LANES))
        for k in range(mine):
            income = (wage[periods - 1] * productivity[core * mine + k]) * level_col[...]
            for b in range(blocks):
                vals[k, :, lanes(b)] = end_gross / (end_rate * grid_block(b) + income)
            live = active[core * mine + k] * BLOCK
            for b in range(blocks):
                start = full_rows(mass_in[k, :, lanes(b)])
                mass[k, :, lanes(b)] = jnp.where(lane_id + b * LANES < live, start, 0.0)

        def backward(step, carry):
            t = periods - 1 - step
            if newton_round == 0:
                pltpu.make_async_copy(
                    brackets.at[pl.ds(0, mine), 0],
                    br.at[t],
                    br_sem.at[t],
                ).wait()
            gross = jnp.broadcast_to(rates[0, pl.ds(t, 1), :], (ROWS, LANES))
            inverse = jnp.broadcast_to(rates[1, pl.ds(t, 1), :], (ROWS, LANES))
            for k in range(mine):
                income = (wage[t] * productivity[core * mine + k]) * level_col[...]
                patient = patience[core * mine + k]
                endogenous = []
                for b in range(blocks):
                    expected = None
                    for f in range(incomes):
                        term = t_back[f] * jnp.broadcast_to(
                            vals[k, pl.ds(f, 1), lanes(b)], (ROWS, LANES)
                        )
                        expected = term if expected is None else expected + term
                    endogenous.append(
                        (1.0 / (patient * expected) + grid_block(b) - income) * inverse
                    )
                for b in range(blocks):
                    j = bracket_block(t, k, b)
                    low_at = jnp.bitwise_and(j, LANES - 1)
                    high_at = jnp.bitwise_and(j + 1, LANES - 1)
                    lower = take(endogenous[b], low_at)
                    upper = take(endogenous[b], high_at)
                    if b > 0:
                        lower = jnp.where(j >= b * LANES, lower, take(endogenous[b - 1], low_at))
                        upper = jnp.where(
                            j + 1 >= b * LANES, upper, take(endogenous[b - 1], high_at)
                        )
                    jf = j.astype(jnp.float32)
                    grid_low = grid_unit * (jf * jf)
                    grid_step = grid_unit * (2.0 * jf + 1.0)
                    grid_here = grid_block(b)
                    spacing = jnp.maximum(upper - lower, grid_step * inverse)
                    weight = jnp.clip((grid_here - lower) / spacing, 0.0, 1.0)
                    saved = grid_low + weight * grid_step
                    spent = gross * grid_here + income - saved
                    weights[t, k, :, lanes(b)] = weight
                    savings[t, k, :, lanes(b)] = saved
                    if last:
                        spending[t, k, :, lanes(b)] = spent
                    vals[k, :, lanes(b)] = gross / spent
            return carry

        lax.fori_loop(0, periods, backward, 0)

        def forward(t, carry):
            for k in range(mine):
                assets_sum = None
                spent_sum = None
                stay, rise, drop = [], [], []
                for b in range(blocks):
                    now = mass[k, :, lanes(b)]
                    held = now * savings[t, k, :, lanes(b)]
                    assets_sum = held if assets_sum is None else assets_sum + held
                    if last:
                        used = now * spending[t, k, :, lanes(b)]
                        spent_sum = used if spent_sum is None else spent_sum + used
                    up = weights[t, k, :, lanes(b)] * now
                    rise.append(up)
                    stay.append(now - up)
                    drop.append(lane_id + b * LANES - bracket_block(t, k, b))
                totals[2 * k, t] = assets_sum
                if last:
                    totals[2 * k + 1, t] = spent_sum
                sums = [None] * blocks
                sums[0] = pltpu.roll(jnp.where(drop[0] == 0, rise[0], 0.0), 1, 1)
                for s in range(REACH + 2):
                    part = [
                        jnp.where(
                            drop[b] == s, stay[b], jnp.where(drop[b] == s + 1, rise[b], 0.0)
                        )
                        for b in range(blocks)
                    ]
                    for b in range(blocks):
                        piece = part[b]
                        if s > 0:
                            above = part[b + 1] if b + 1 < blocks else jnp.zeros_like(piece)
                            piece = shifted(jnp.where(lane_id >= s, piece, above), s)
                        sums[b] = piece if sums[b] is None else sums[b] + piece
                for b in range(blocks):
                    arrived[k, :, lanes(b)] = sums[b]
                for b in range(blocks):
                    new = None
                    for e in range(incomes):
                        term = t_fwd[e] * jnp.broadcast_to(
                            arrived[k, pl.ds(e, 1), lanes(b)], (ROWS, LANES)
                        )
                        new = term if new is None else new + term
                    mass[k, :, lanes(b)] = new
            return carry

        lax.fori_loop(0, periods, forward, 0)

        row = jnp.zeros((1, LANES), jnp.float32)
        if last:
            for c in range(2 * mine):
                series = jnp.sum(totals[c], axis=1)
                row = row + to_row(jnp.sum(series, axis=1, keepdims=True), c * periods)
        else:
            series = totals[0]
            for k in range(1, mine):
                series = series + totals[2 * k]
            series = jnp.sum(series, axis=1)
            row = to_row(jnp.sum(series, axis=1, keepdims=True), 0)
        inbox = recv_b if last else recv_a
        send_row[newton_round] = row
        inbox[me] = row

        def row_copy(o):
            return pltpu.make_async_remote_copy(
                src_ref=send_row.at[newton_round],
                dst_ref=inbox.at[me],
                send_sem=row_send.at[newton_round],
                recv_sem=row_recv.at[newton_round],
                device_id=place(lax.rem(me + o, devices)),
                device_id_type=MESH,
            )

        def send(o, carry):
            row_copy(o).start()
            return carry

        lax.fori_loop(1, devices, send, 0)
        others = inbox.at[pl.ds(0, devices - 1)]
        pltpu.make_async_copy(others, others, row_recv.at[newton_round]).wait()
        total = jnp.sum(inbox[0:devices], axis=0)
        if last:
            total = functools.reduce(
                jnp.add, [shifted(total, 2 * k * periods) for k in range(mine)]
            )
        gap = jnp.where(
            lane_id[0:1] < periods, total / float(groups * local_types) - bond_row, 0.0
        )
        change = jnp.sum(
            jac[...] * jnp.broadcast_to(gap[:, 0:periods], (periods, periods)),
            axis=1,
            keepdims=True,
        )
        price = price - to_row(change, 0)
        pltpu.make_async_copy(others, others, row_send.at[newton_round]).wait()

    price_out[...] = price[:, 0:periods]
    gap_out[...] = gap[:, 0:periods]
    for s in range(local_types):
        wanted = assignment[group * local_types + s]
        source = recv_b[wanted // mine]
        within = lax.rem(wanted, mine)
        found = source
        for k in range(1, mine):
            found = jnp.where(within == k, shifted(source, 2 * k * periods), found)
        paths_out[s, 0:1, :] = found[:, 0:periods]
        paths_out[s, 1:2, :] = shifted(found, periods)[:, 0:periods]

    for p in range(here):
        for o in range(1, cores):
            peer_copy(o, p).wait_send()


def body(groups, cores, *args):
    brackets, assignment = args[0], args[-1]
    local_types, here, incomes, assets = brackets.shape
    periods = here * cores
    mine = local_types // cores
    devices = groups * cores
    sizes = (groups, cores, local_types, periods, incomes, assets)
    assert 2 * mine * periods <= LANES and periods == ROWS and incomes <= ROWS
    args = list(args)
    args[8] = args[8].reshape(1, periods)
    args[9] = args[9].reshape(1, periods)
    vmem = pl.BlockSpec(memory_space=pltpu.VMEM)
    smem = pl.BlockSpec(memory_space=pltpu.SMEM)
    far = pl.BlockSpec(memory_space=pl.ANY)
    f32 = jnp.float32
    per_period = pltpu.VMEM((periods, mine, ROWS, assets), f32)
    per_type = pltpu.VMEM((mine + 1, ROWS, assets), f32)
    price, gap, paths = pl.pallas_call(
        functools.partial(kernel, sizes),
        out_shape=(
            jax.ShapeDtypeStruct((1, periods), f32),
            jax.ShapeDtypeStruct((1, periods), f32),
            jax.ShapeDtypeStruct((local_types, 2, periods), f32),
        ),
        in_specs=[far, smem, far, smem, smem, smem, smem, smem, vmem, vmem, vmem, smem],
        out_specs=(vmem, vmem, vmem),
        scratch_shapes=[
            pltpu.VMEM((periods, mine, incomes, assets), jnp.int32),
            pltpu.VMEM((mine, incomes, assets), f32),
            per_type, per_type, per_type,
            per_period, per_period, per_period,
            pltpu.VMEM((2 * mine, periods, ROWS, LANES), f32),
            pltpu.VMEM((incomes, ROWS, LANES), f32),
            pltpu.VMEM((incomes, ROWS, LANES), f32),
            pltpu.VMEM((ROWS, LANES), f32),
            pltpu.VMEM((3, ROWS, LANES), f32),
            pltpu.VMEM((NEWTON + ROWS, 1, LANES), f32),
            pltpu.VMEM((devices + ROWS, 1, LANES), f32),
            pltpu.VMEM((devices + ROWS, 1, LANES), f32),
            pltpu.SemaphoreType.DMA((periods,)),
            pltpu.SemaphoreType.DMA((cores - 1, here)),
            pltpu.SemaphoreType.DMA((1,)),
            pltpu.SemaphoreType.DMA((NEWTON,)),
            pltpu.SemaphoreType.DMA((NEWTON,)),
        ],
        compiler_params=pltpu.CompilerParams(collective_id=0, has_side_effects=True),
    )(*args)
    return price.reshape(periods), gap.reshape(periods), paths


def solution(mesh):
    placed = (
        P("types", "tm", None, None),
        P("types"),
        P("types", None, None),
        P("types"),
        P("types"),
        P(),
        P(),
        P(),
        P(),
        P(),
        P(),
        P(),
    )
    return jax.shard_map(
        functools.partial(body, mesh.shape["types"], mesh.shape["tm"]),
        mesh=mesh,
        in_specs=placed,
        out_specs=(P(), P(), P("types", None, None)),
        check_vma=False,
    )
```

time: 973 us -> 31.7 us (0.03); the launches traced: 990 us -> 31.5 us
  loops' own time: 321 us -> 0 us
  blocking collectives: 207 us -> 0 us
  matrix products: 204 us -> 0 us
  other arithmetic: 140 us -> 0 us
  local copies, waits for them, and re-layouts: 111 us -> 4.27 us
  Pallas kernels: 0 us -> 26.5 us
    another operation x112 -> x0, loops' own time: 321 us -> none  [the longest x48 144 us: forward_period(): lax.fori_loop(0, blocks, forward_block_rows, jnp.zeros_like(weights))]
    dot_general x419 -> x0, matrix products: 204 us -> none  [the longest x160 88.8 us: backward_block_rows(): jnp.einsum('eia,cea->cei', onehot, stacked_window, precision=highest)]
    psum x2 -> x0, blocking collectives: 124 us -> none  [body(): totals = lax.psum(local_sum, ('types', 'tm'))]
    all_gather x1 -> x0, blocking collectives: 83 us -> none  [body(): lax.all_gather(solve_type_series, ('types', 'tm'), axis=0, tiled=True)]
    broadcast_in_dim x48 -> x0, other arithmetic: 64.1 us -> none  [forward_type(): lax.scan(forward_period, mass_start, (bracket, weight_up, savings, spendi...]
    dynamic_update_slice x322 -> x0, local copies, waits for them, and re-layouts: 43.9 us -> none  [the longest x160 41.4 us: forward_block_rows(): lax.dynamic_update_slice_in_dim(shifted_mass, current + contrib, window, 2)]
    dynamic_slice x387 -> x0, local copies, waits for them, and re-layouts: 42.2 us -> none  [the longest x48 28.3 us: backward_type(): lax.scan(backward_period, values_end, (bracket, interest_path, incomes),...]
    reduce_sum x50 -> x0, other arithmetic: 32.5 us -> none  [the longest x48 32.5 us: forward_period(): jnp.sum(masses * savings_now)]
  transfers between devices with their start and end apart: 1 -> 0, of which waited for: 0 -> 0; matrix products, arithmetic and copies ran while one was open for 0% -> 0% of each run, Pallas kernels for 0% -> 0%
where the time goes in v1:
time: 31.7 us; the launch traced here: 31.5 us
  Pallas kernels  26.5 us (84%)
  local copies, waits for them, and re-layouts  4.27 us (13%)
  between operations  0.66 us (2%)
    pallas_call x1, Pallas kernels, body(): pl.pallas_call(functools.partial(kernel, sizes), out_shape=(jax.ShapeDtyp...  26.5 us
    unnamed x10, local copies, waits for them, and re-layouts  4.27 us

profile of v1, /device:TPU:0, one launch (start us, length us, event | category | flops | bytes accessed | tf_op | source)
XLA Modules:
  0.0 31.5 jit_solution(1852982791468229140)
XLA Ops:
  0.6 1.9 %copy.15.brackets = s32[6,4,7,512]{3,2,1,0:T(8,128)} copy(s32[6,4,7,512]{3,1,2,0:T(4,128)} %param.12) | data formatting | bytes 688128 | tf_op args[0]
  2.5 26.5 %shard_map.139 = (f32[1,8]{1,0:T(1,128)}, f32[1,8]{1,0:T(1,128)}, f32[6,2,8]{2,1,0:T(2,128)}) custom-call(s32[6,4,7,512]{3,2,1,0:T(8,128)} %copy.15.brackets, s32[6]{0:T(128)} %active.1, f32[6,7,512]{2,1,0:T(8,128)} %initial_mass.1, f32[6]{0:T(128)} %patience.1, f32[6]{0:T(128)} %productivity.1, f32[7]{0:T(128)} %levels.1, f32[7,7]{1,0:T(8,128)} %transition.1, ...), custom_call_target="tpu_custom_call" | custom-call | tf_op jit(solution)/shard_map/pallas_call | solution.py:340
  29.0 0.0 copy-start
  29.1 0.0 copy-start.2
  29.1 0.7 %copy-done.2 = f32[1,8]{1,0:T(1,128)S(1)} copy-done((f32[1,8]{1,0:T(1,128)S(1)}, f32[1,8]{1,0:T(1,128)}, u32[]{:S(2)}) %copy-start.2) | copy-done | bytes 56
  29.7 0.0 copy-start.1
  29.7 0.5 %copy.19 = f32[8]{0:T(128)} copy(f32[8]{0:T(128)S(1)} %bitcast.7) | data formatting | bytes 64
  30.3 0.1 copy-done.1
  30.4 0.5 %copy.20 = f32[8]{0:T(128)} copy(f32[8]{0:T(128)S(1)} %bitcast.6) | data formatting | bytes 64
  30.9 0.0 copy-done
  30.9 0.6 %copy.21 = f32[6,2,8]{2,1,0:T(2,128)} copy(f32[6,2,8]{2,1,0:T(2,128)S(1)} %copy-done) | data formatting | bytes 768
Async XLA Ops:
  29.0 1.8 %copy-start = (f32[6,2,8]{2,1,0:T(2,128)S(1)}, f32[6,2,8]{2,1,0:T(2,128)}, u32[]{:S(2)}) copy-start(f32[6,2,8]{2,1,0:T(2,128)} %get-tuple-element.14) | copy-start | bytes 1156
  29.1 0.7 %copy-start.2 = (f32[1,8]{1,0:T(1,128)S(1)}, f32[1,8]{1,0:T(1,128)}, u32[]{:S(2)}) copy-start(f32[1,8]{1,0:T(1,128)} %get-tuple-element.6) | copy-start | bytes 100
  29.7 0.6 %copy-start.1 = (f32[1,8]{1,0:T(1,128)S(1)}, f32[1,8]{1,0:T(1,128)}, u32[]{:S(2)}) copy-start(f32[1,8]{1,0:T(1,128)} %get-tuple-element.7) | copy-start | bytes 100

commit v2 on v1

--- a/solution.py
+++ b/solution.py
@@ -65,7 +65,7 @@
 
     def local_copy(p):
         return pltpu.make_async_copy(
-            brackets.at[pl.ds(core * mine, mine), p],
+            brackets.at[pl.ds(core * mine, mine), :, p],
             br.at[core * here + p],
             br_sem.at[core * here + p],
         )
@@ -109,7 +109,7 @@
     def peer_copy(o, p):
         peer = lax.rem(core + o, cores)
         return pltpu.make_async_remote_copy(
-            src_ref=brackets.at[pl.ds(peer * mine, mine), p],
+            src_ref=brackets.at[pl.ds(peer * mine, mine), :, p],
             dst_ref=br.at[core * here + p],
             send_sem=br_send.at[o - 1, p],
             recv_sem=br_sem.at[core * here + p],
@@ -159,7 +159,7 @@
             t = periods - 1 - step
             if newton_round == 0:
                 pltpu.make_async_copy(
-                    brackets.at[pl.ds(0, mine), 0],
+                    brackets.at[pl.ds(0, mine), :, 0],
                     br.at[t],
                     br_sem.at[t],
                 ).wait()
@@ -320,6 +320,12 @@
             peer_copy(o, p).wait_send()
 
 
+def hand_out(price, gap, paths, price_out, gap_out, paths_out):
+    price_out[...] = price[...]
+    gap_out[...] = gap[...]
+    paths_out[...] = paths[...]
+
+
 def body(groups, cores, *args):
     brackets, assignment = args[0], args[-1]
     local_types, here, incomes, assets = brackets.shape
@@ -329,6 +335,7 @@
     sizes = (groups, cores, local_types, periods, incomes, assets)
     assert 2 * mine * periods <= LANES and periods == ROWS and incomes <= ROWS
     args = list(args)
+    args[0] = jnp.transpose(brackets, (0, 2, 1, 3))
     args[8] = args[8].reshape(1, periods)
     args[9] = args[9].reshape(1, periods)
     vmem = pl.BlockSpec(memory_space=pltpu.VMEM)
@@ -367,6 +374,12 @@
         ],
         compiler_params=pltpu.CompilerParams(collective_id=0, has_side_effects=True),
     )(*args)
+    price, gap, paths = pl.pallas_call(
+        hand_out,
+        out_shape=tuple(jax.ShapeDtypeStruct(x.shape, f32) for x in (price, gap, paths)),
+        in_specs=[vmem] * 3,
+        out_specs=(vmem,) * 3,
+    )(price, gap, paths)
     return price.reshape(periods), gap.reshape(periods), paths
 
 

time: 31.7 us -> 28.7 us (0.905)
  local copies, waits for them, and re-layouts: 4.27 us -> 0 us
  Pallas kernels: 26.5 us -> 27.9 us
    unnamed x10 -> x0, local copies, waits for them, and re-layouts: 4.27 us -> none
    pallas_call x0 -> x1, Pallas kernels: none -> 1.31 us  [body(): pl.pallas_call(hand_out, out_shape=tuple((jax.ShapeDtypeStruct(x.shape, f...]
where the time goes in v2:
time: 28.7 us; the launch traced here: 28.5 us
  Pallas kernels  27.9 us (97%)
  between operations  0.64 us (2%)
    pallas_call x1, Pallas kernels, body(): pl.pallas_call(functools.partial(kernel, sizes), out_shape=(jax.ShapeDtyp...  26.6 us
    pallas_call x1, Pallas kernels, body(): pl.pallas_call(hand_out, out_shape=tuple((jax.ShapeDtypeStruct(x.shape, f...  1.31 us

profile of v2, /device:TPU:0, one launch (start us, length us, event | category | flops | bytes accessed | tf_op | source)
XLA Modules:
  0.0 28.5 jit_solution(18365072095823367175)
XLA Ops:
  0.6 26.6 %shard_map.139 = (f32[1,8]{1,0:T(1,128)}, f32[1,8]{1,0:T(1,128)}, f32[6,2,8]{2,1,0:T(2,128)}) custom-call(s32[6,7,4,512]{3,2,1,0:T(4,128)} %bitcast.5, s32[6]{0:T(128)} %active.1, f32[6,7,512]{2,1,0:T(8,128)} %initial_mass.1, f32[6]{0:T(128)} %patience.1, f32[6]{0:T(128)} %productivity.1, f32[7]{0:T(128)} %levels.1, f32[7,7]{1,0:T(8,128)} %transition.1, ...), custom_call_target="tpu_custom_call" | custom-call | tf_op jit(solution)/shard_map/pallas_call | solution.py:347
  27.2 1.3 %shard_map.140 = (f32[1,8]{1,0:T(1,128)}, f32[1,8]{1,0:T(1,128)}, f32[6,2,8]{2,1,0:T(2,128)}) custom-call(f32[1,8]{1,0:T(1,128)} %get-tuple-element.9.price, f32[1,8]{1,0:T(1,128)} %get-tuple-element.10.gap, f32[6,2,8]{2,1,0:T(2,128)} %get-tuple-element.11.paths), custom_call_target="tpu_custom_call" | custom-call | tf_op jit(solution)/shard_map/pallas_call | solution.py:377
